TPU v7x, 512 devices: a whole 4x8x8 slice. The times are simulated.
512 devices in a mesh: grp: 16 (over y, core), mem: 32 (over x, z).
Axes of the slice: x: 4, y: 8, z: 8, core: 2. Of those that a mesh axis runs over, the one named last changes fastest.
Arguments:
- v_stack: bfloat16 [524288, 512], P(('grp', 'mem')), may hold values from -0.1875 to 0.1875
- u_stack: bfloat16 [524288, 512], P(('grp', 'mem')), may hold values from -0.25 to 0.25
- warm_start: bfloat16 [524288, 256], P(('grp', 'mem')), may hold values from -3 to 3
- observed: bfloat16 [524288, 256], P(('grp', 'mem')), may hold values from -12 to 12, as said below
- owners: int32 [512, 4], replicated, may hold values from 0 to 511, as said below
- tile_ranks: int32 [512, 4], P(('grp', 'mem')), may hold values from 8 to 128
Outputs:
- model: float32 [524288, 256], P(('grp', 'mem'))
- residual: bfloat16 [524288, 256], P(('grp', 'mem'))
Inputs may be any that keep to these rules, and one draw needn't show every extreme that they name: Writing d = g * 32 + m, owners[d, t] = ((g + a_t) mod 16) * 32 + (m + b_t) mod 32, where the offsets a_t differ over t, the offsets b_t differ over t, some slot has a_t = 15, some slot has a_t = 8, some slot has b_t = 31 and some slot has b_t = 16. `observed`: entries of one row block share a scale.
All inputs are finite; a program needn't handle non-finite values.
Results may differ from a plain program's by a relative error of at most 0.006.
Values may be sent and summed in bfloat16 or wider, within the bound.
No kernel may reach another device: no remote copies, remote signals or barrier semaphores. Data moves between devices by JAX's collectives and lax.ppermute only.
A program may use at most 64 MiB of HBM per device.

v0:
```python
import jax
import jax.numpy as jnp
from jax import lax
from jax.sharding import Mesh
from jax.sharding import PartitionSpec as P

ITERS = 2
GRP = ("grp_0", "grp_1")
MEM = ("mem_0", "mem_1")
GRP_MEM = ("grp_0", "grp_1", "mem_0", "mem_1")


def one_axis_at_a_time(x, axes):
    for axis in axes:
        x = lax.psum(x, axis)
    return x


def pack_panels(panels, targets, peers):
    placing = (targets[:, None] == jnp.arange(peers, dtype=jnp.int32)[None, :]).astype(jnp.bfloat16)
    return jnp.einsum("tk,trh->krh", placing, panels, preferred_element_type=jnp.float32).astype(
        jnp.bfloat16
    )


def unpack_panels(received, chosen):
    return jnp.einsum(
        "kt,krh->trh", chosen.astype(jnp.bfloat16), received, preferred_element_type=jnp.float32
    ).astype(jnp.bfloat16)


def cross_groups(panels, group_steps):
    peers = lax.axis_size(GRP)
    own_group = lax.axis_index(GRP)
    outgoing = pack_panels(panels, (own_group + group_steps) % peers, peers)
    received = lax.all_to_all(outgoing, GRP, split_axis=0, concat_axis=0, tiled=True)
    anchors = (
        jnp.arange(peers, dtype=jnp.int32)[:, None] + group_steps[None, :]
    ) % peers == own_group
    return unpack_panels(received, anchors)


def cross_members(panels, member_steps):
    peers = lax.axis_size(MEM)
    own_member = lax.axis_index(MEM)
    outgoing = pack_panels(panels, (own_member + member_steps) % peers, peers)
    received = lax.all_to_all(outgoing, MEM, split_axis=0, concat_axis=0, tiled=True)
    anchors = (
        jnp.arange(peers, dtype=jnp.int32)[:, None] + member_steps[None, :]
    ) % peers == own_member
    return unpack_panels(received, anchors)


def route_panels(panels, group_steps, member_steps):
    moved = cross_groups(panels, group_steps)
    return cross_members(moved, member_steps)


def on_device(v_stack, u_stack, warm_start, observed, owners, tile_ranks):
    group_count = lax.axis_size(GRP)
    member_count = lax.axis_size(MEM)
    slots_held = owners.shape[1]
    stack_width = v_stack.shape[1]
    rank_cap = stack_width // slots_held
    right_count = warm_start.shape[1]
    live_rows = (
        lax.broadcasted_iota(jnp.int32, (slots_held, rank_cap), 1) < tile_ranks[0][:, None]
    ).astype(jnp.float32)
    forward_groups = owners[0] // member_count % group_count
    forward_members = owners[0] % member_count
    backward_groups = (group_count - forward_groups) % group_count
    backward_members = (member_count - forward_members) % member_count

    def forward(field):
        panels = jnp.einsum("bk,bh->kh", v_stack, field, preferred_element_type=jnp.float32)
        panels = (panels.reshape(slots_held, rank_cap, right_count) * live_rows[:, :, None]).astype(
            jnp.bfloat16
        )
        arrived = route_panels(panels, forward_groups, forward_members)
        return jnp.dot(
            u_stack, arrived.reshape(stack_width, right_count), preferred_element_type=jnp.float32
        )

    def adjoint(field):
        panels = jnp.einsum("bk,bh->kh", u_stack, field, preferred_element_type=jnp.float32)
        panels = panels.reshape(slots_held, rank_cap, right_count).astype(jnp.bfloat16)
        returned = route_panels(panels, backward_groups, backward_members)
        masked = (returned * live_rows[:, :, None]).astype(jnp.bfloat16)
        return jnp.dot(
            v_stack, masked.reshape(stack_width, right_count), preferred_element_type=jnp.float32
        )

    model = warm_start.astype(jnp.float32)
    residual = forward(warm_start) - observed.astype(jnp.float32)
    entries = float(warm_start.shape[0] * right_count * group_count * member_count)

    def iterate(index, carry):
        model, residual = carry
        spread = one_axis_at_a_time(jnp.sum(jnp.abs(residual)), GRP_MEM)
        huber_scale = 1.345 * spread / entries + 1e-06
        weights = huber_scale / jnp.maximum(jnp.abs(residual), huber_scale)
        weighted = (weights * residual).astype(jnp.bfloat16)
        gradient = adjoint(weighted)
        grad_sum = one_axis_at_a_time(jnp.sum(gradient * gradient), GRP_MEM)
        image_dir = forward(gradient.astype(jnp.bfloat16))
        curve_sum = one_axis_at_a_time(jnp.sum(weights * image_dir * image_dir), GRP_MEM)
        step_size = grad_sum / (curve_sum + 1e-06)
        return (model - step_size * gradient, residual - step_size * image_dir)

    model, residual = lax.fori_loop(0, ITERS, iterate, (model, residual))
    return (model, residual.astype(jnp.bfloat16))


def solution(mesh):
    finer = Mesh(mesh.devices.reshape(8, 2, 4, 8), ("grp_0", "grp_1", "mem_0", "mem_1"))
    placed = (
        P(GRP_MEM, None),
        P(GRP_MEM, None),
        P(GRP_MEM, None),
        P(GRP_MEM, None),
        P(),
        P(GRP_MEM, None),
    )
    return jax.shard_map(
        on_device,
        mesh=finer,
        in_specs=placed,
        out_specs=(P(GRP_MEM, None), P(GRP_MEM, None)),
        check_vma=False,
    )
```

profile of v0, /device:TPU:8, one launch (start us, length us, event | category | flops | bytes accessed | tf_op | source)
XLA Modules:
  0.0 714.6 jit_solution(6937026796179106969)
XLA Ops:
  6.2 9.2 %all-to-all-start.4 = ((bf16[16,128,256]{2,1,0:T(8,128)(2,1)}), bf16[16,128,256]{2,1,0:T(8,128)(2,1)S(1)}, u32[]{:S(2)}, u32[]{:S(2)}) async-start(bf16[16,128,256]{2,1,0:T(8,128)(2,1)} %copy.53), calls=%async_computation.4 | async-start | bytes 2097152 | tf_op jit(solution)/shard_map/all_to_all | solution.py:36
  15.5 24.6 %all-to-all-done.4 = bf16[16,128,256]{2,1,0:T(8,128)(2,1)S(1)} async-done(((bf16[16,128,256]{2,1,0:T(8,128)(2,1)}), bf16[16,128,256]{2,1,0:T(8,128)(2,1)S(1)}, u32[]{:S(2)}, u32[]{:S(2)}) %all-to-all-start.4) | async-done | bytes 1048608 | tf_op jit(solution)/shard_map/all_to_all | solution.py:36
  43.9 11.6 %all-to-all-start.5 = ((bf16[32,128,256]{2,1,0:T(8,128)(2,1)}), bf16[32,128,256]{2,1,0:T(8,128)(2,1)S(1)}, u32[]{:S(2)}, u32[]{:S(2)}) async-start(bf16[32,128,256]{2,1,0:T(8,128)(2,1)} %copy.55), calls=%async_computation.5 | async-start | bytes 4194304 | tf_op jit(solution)/shard_map/all_to_all | solution.py:47
  58.9 47.2 %all-to-all-done.5 = bf16[32,128,256]{2,1,0:T(8,128)(2,1)S(1)} async-done(((bf16[32,128,256]{2,1,0:T(8,128)(2,1)}), bf16[32,128,256]{2,1,0:T(8,128)(2,1)S(1)}, u32[]{:S(2)}, u32[]{:S(2)}) %all-to-all-start.5) | async-done | bytes 2097184 | tf_op jit(solution)/shard_map/all_to_all | solution.py:47
  110.1 599.7 %while.16 = (s32[]{:T(128)}, f32[1024,256]{0,1:T(8,128)}, f32[1024,256]{0,1:T(8,128)}, s32[4]{0:T(128)S(1)}, s32[4]{0:T(128)S(1)}, /*index=5*/bf16[1024,512]{1,0...) while((s32[]{:T(128)}, f32[1024,256]{0,1:T(8,128)}, ...), condition=%wide.region_16.17_spmd.clone, body=%wide.region_0.16_spmd.clone.sunk | while | flops 1133779456 | bytes 70786008 | solution.py:110
  112.2 16.6 %psum.148 = f32[]{:T(128)} all-reduce(f32[]{:T(128)} %abs_reduce_fusion.2), channel_id=1, replica_groups=mesh['grp_0'=8,'grp_1'=2,'mem_0'=4,'mem_1'=8] {'grp_0'}, use_global_device_ids=true, to_apply=%region_2.2 | all-reduce | flops 1 | bytes 8 | tf_op jit(solution)/shard_map/while/body/eval_jaxpr/psum | solution.py:15
  131.9 9.2 %psum.150 = f32[]{:T(128)} all-reduce(f32[]{:T(128)} %psum.149), channel_id=1, replica_groups=mesh['grp_0'=8,'grp_1'=2,'mem_0'=4,'mem_1'=8] {'mem_0'}, use_global_device_ids=true, to_apply=%region_4.4 | all-reduce | flops 1 | bytes 8 | tf_op jit(solution)/shard_map/while/body/eval_jaxpr/psum | solution.py:15
  141.1 18.6 %psum.151 = f32[]{:T(128)} all-reduce(f32[]{:T(128)} %psum.150), channel_id=1, replica_groups=mesh['grp_0'=8,'grp_1'=2,'mem_0'=4,'mem_1'=8] {'mem_1'}, use_global_device_ids=true, to_apply=%region_5.5 | all-reduce | flops 1 | bytes 8 | tf_op jit(solution)/shard_map/while/body/eval_jaxpr/psum | solution.py:15
  170.6 24.7 %all-to-all-done = bf16[16,128,256]{2,1,0:T(8,128)(2,1)} async-done(((bf16[16,128,256]{2,1,0:T(8,128)(2,1)}), bf16[16,128,256]{2,1,0:T(8,128)(2,1)}, u32[]{:S(2)}, u32[]{:S(2)}) %all-to-all-start) | async-done | bytes 1048608 | tf_op jit(solution)/shard_map/while/body/eval_jaxpr/all_to_all | solution.py:36
  206.2 50.5 %all-to-all-done.1 = bf16[32,128,256]{2,1,0:T(8,128)(2,1)S(1)} async-done(((bf16[32,128,256]{2,1,0:T(8,128)(2,1)}), bf16[32,128,256]{2,1,0:T(8,128)(2,1)S(1)}, u32[]{:S(2)}, u32[]{:S(2)}) %all-to-all-start.1) | async-done | bytes 2097184 | tf_op jit(solution)/shard_map/while/body/eval_jaxpr/all_to_all | solution.py:47
  268.7 24.7 %all-to-all-done.2 = bf16[16,128,256]{2,1,0:T(8,128)(2,1)} async-done(((bf16[16,128,256]{2,1,0:T(8,128)(2,1)}), bf16[16,128,256]{2,1,0:T(8,128)(2,1)}, u32[]{:S(2)}, u32[]{:S(2)}) %all-to-all-start.2) | async-done | bytes 1048608 | tf_op jit(solution)/shard_map/while/body/eval_jaxpr/all_to_all | solution.py:36
  305.3 50.5 %all-to-all-done.3 = bf16[32,128,256]{2,1,0:T(8,128)(2,1)S(1)} async-done(((bf16[32,128,256]{2,1,0:T(8,128)(2,1)}), bf16[32,128,256]{2,1,0:T(8,128)(2,1)S(1)}, u32[]{:S(2)}, u32[]{:S(2)}) %all-to-all-start.3) | async-done | bytes 2097184 | tf_op jit(solution)/shard_map/while/body/eval_jaxpr/all_to_all | solution.py:47
  359.8 16.8 %all-reduce.8 = (f32[]{:T(128)}, f32[]{:T(128)}) all-reduce(f32[]{:T(128)} %get-tuple-element.315, f32[]{:T(128)} %get-tuple-element.316), channel_id=1, replica_groups=mesh['grp_0'=8,'grp_1'=2,'mem_0'=4,'mem_1'=8] {'grp_0'}, use_global_device_ids=true, to_apply=%region_7.7 | all-reduce | flops 2 | bytes 16 | tf_op jit(solution)/shard_map/while/body/eval_jaxpr/psum | solution.py:15
  379.7 9.5 %all-reduce.10 = (f32[]{:T(128)}, f32[]{:T(128)}) all-reduce(f32[]{:T(128)} %get-tuple-element.319, f32[]{:T(128)} %get-tuple-element.320), channel_id=1, replica_groups=mesh['grp_0'=8,'grp_1'=2,'mem_0'=4,'mem_1'=8] {'mem_0'}, use_global_device_ids=true, to_apply=%region_9.9 | all-reduce | flops 2 | bytes 16 | tf_op jit(solution)/shard_map/while/body/eval_jaxpr/psum | solution.py:15
  389.2 18.3 %all-reduce.11 = (f32[]{:T(128)}, f32[]{:T(128)}) all-reduce(f32[]{:T(128)} %get-tuple-element.321, f32[]{:T(128)} %get-tuple-element.322), channel_id=1, replica_groups=mesh['grp_0'=8,'grp_1'=2,'mem_0'=4,'mem_1'=8] {'mem_1'}, use_global_device_ids=true, to_apply=%region_10.10 | all-reduce | flops 2 | bytes 16 | tf_op jit(solution)/shard_map/while/body/eval_jaxpr/psum | solution.py:15
  414.2 14.8 %psum.148 = f32[]{:T(128)} all-reduce(f32[]{:T(128)} %abs_reduce_fusion.2), channel_id=1, replica_groups=mesh['grp_0'=8,'grp_1'=2,'mem_0'=4,'mem_1'=8] {'grp_0'}, use_global_device_ids=true, to_apply=%region_2.2 | all-reduce | flops 1 | bytes 8 | tf_op jit(solution)/shard_map/while/body/eval_jaxpr/psum | solution.py:15
  440.4 15.6 %psum.151 = f32[]{:T(128)} all-reduce(f32[]{:T(128)} %psum.150), channel_id=1, replica_groups=mesh['grp_0'=8,'grp_1'=2,'mem_0'=4,'mem_1'=8] {'mem_1'}, use_global_device_ids=true, to_apply=%region_5.5 | all-reduce | flops 1 | bytes 8 | tf_op jit(solution)/shard_map/while/body/eval_jaxpr/psum | solution.py:15
  467.6 24.7 %all-to-all-done = bf16[16,128,256]{2,1,0:T(8,128)(2,1)} async-done(((bf16[16,128,256]{2,1,0:T(8,128)(2,1)}), bf16[16,128,256]{2,1,0:T(8,128)(2,1)}, u32[]{:S(2)}, u32[]{:S(2)}) %all-to-all-start) | async-done | bytes 1048608 | tf_op jit(solution)/shard_map/while/body/eval_jaxpr/all_to_all | solution.py:36
  504.0 50.5 %all-to-all-done.1 = bf16[32,128,256]{2,1,0:T(8,128)(2,1)S(1)} async-done(((bf16[32,128,256]{2,1,0:T(8,128)(2,1)}), bf16[32,128,256]{2,1,0:T(8,128)(2,1)S(1)}, u32[]{:S(2)}, u32[]{:S(2)}) %all-to-all-start.1) | async-done | bytes 2097184 | tf_op jit(solution)/shard_map/while/body/eval_jaxpr/all_to_all | solution.py:47
  566.4 24.7 %all-to-all-done.2 = bf16[16,128,256]{2,1,0:T(8,128)(2,1)} async-done(((bf16[16,128,256]{2,1,0:T(8,128)(2,1)}), bf16[16,128,256]{2,1,0:T(8,128)(2,1)}, u32[]{:S(2)}, u32[]{:S(2)}) %all-to-all-start.2) | async-done | bytes 1048608 | tf_op jit(solution)/shard_map/while/body/eval_jaxpr/all_to_all | solution.py:36
  603.0 50.5 %all-to-all-done.3 = bf16[32,128,256]{2,1,0:T(8,128)(2,1)S(1)} async-done(((bf16[32,128,256]{2,1,0:T(8,128)(2,1)}), bf16[32,128,256]{2,1,0:T(8,128)(2,1)S(1)}, u32[]{:S(2)}, u32[]{:S(2)}) %all-to-all-start.3) | async-done | bytes 2097184 | tf_op jit(solution)/shard_map/while/body/eval_jaxpr/all_to_all | solution.py:47
  657.6 16.8 %all-reduce.8 = (f32[]{:T(128)}, f32[]{:T(128)}) all-reduce(f32[]{:T(128)} %get-tuple-element.315, f32[]{:T(128)} %get-tuple-element.316), channel_id=1, replica_groups=mesh['grp_0'=8,'grp_1'=2,'mem_0'=4,'mem_1'=8] {'grp_0'}, use_global_device_ids=true, to_apply=%region_7.7 | all-reduce | flops 2 | bytes 16 | tf_op jit(solution)/shard_map/while/body/eval_jaxpr/psum | solution.py:15
  677.4 9.5 %all-reduce.10 = (f32[]{:T(128)}, f32[]{:T(128)}) all-reduce(f32[]{:T(128)} %get-tuple-element.319, f32[]{:T(128)} %get-tuple-element.320), channel_id=1, replica_groups=mesh['grp_0'=8,'grp_1'=2,'mem_0'=4,'mem_1'=8] {'mem_0'}, use_global_device_ids=true, to_apply=%region_9.9 | all-reduce | flops 2 | bytes 16 | tf_op jit(solution)/shard_map/while/body/eval_jaxpr/psum | solution.py:15
  687.0 18.3 %all-reduce.11 = (f32[]{:T(128)}, f32[]{:T(128)}) all-reduce(f32[]{:T(128)} %get-tuple-element.321, f32[]{:T(128)} %get-tuple-element.322), channel_id=1, replica_groups=mesh['grp_0'=8,'grp_1'=2,'mem_0'=4,'mem_1'=8] {'mem_1'}, use_global_device_ids=true, to_apply=%region_10.10 | all-reduce | flops 2 | bytes 16 | tf_op jit(solution)/shard_map/while/body/eval_jaxpr/psum | solution.py:15
  (95 shorter events, 152.4 us)
Async XLA Ops:
  6.2 33.9 %all-to-all-start.4 = ((bf16[16,128,256]{2,1,0:T(8,128)(2,1)}), bf16[16,128,256]{2,1,0:T(8,128)(2,1)S(1)}, u32[]{:S(2)}, u32[]{:S(2)}) async-start(bf16[16,128,256]{2,1,0:T(8,128)(2,1)} %copy.53), calls=%async_computation.4 | async-start | bytes 2097152 | tf_op jit(solution)/shard_map/all_to_all | solution.py:36
  43.9 11.6 %copy-start.3 = (bf16[1024,256]{1,0:T(8,128)(2,1)S(1)}, bf16[1024,256]{1,0:T(8,128)(2,1)}, u32[]{:S(2)}) copy-start(bf16[1024,256]{1,0:T(8,128)(2,1)} %param.10) | copy-start | bytes 1572868
  43.9 62.1 %all-to-all-start.5 = ((bf16[32,128,256]{2,1,0:T(8,128)(2,1)}), bf16[32,128,256]{2,1,0:T(8,128)(2,1)S(1)}, u32[]{:S(2)}, u32[]{:S(2)}) async-start(bf16[32,128,256]{2,1,0:T(8,128)(2,1)} %copy.55), calls=%async_computation.5 | async-start | bytes 4194304 | tf_op jit(solution)/shard_map/all_to_all | solution.py:47
  106.0 1.3 copy-start.2
  107.3 2.8 copy-start
  107.3 2.8 copy-start.4
  164.6 30.8 %all-to-all-start = ((bf16[16,128,256]{2,1,0:T(8,128)(2,1)}), bf16[16,128,256]{2,1,0:T(8,128)(2,1)}, u32[]{:S(2)}, u32[]{:S(2)}) async-start(bf16[16,128,256]{2,1,0:T(8,128)(2,1)} %copy.115), calls=%async_computation | async-start | bytes 2097152 | tf_op jit(solution)/shard_map/while/body/eval_jaxpr/all_to_all | solution.py:36
  200.3 56.4 %all-to-all-start.1 = ((bf16[32,128,256]{2,1,0:T(8,128)(2,1)}), bf16[32,128,256]{2,1,0:T(8,128)(2,1)S(1)}, u32[]{:S(2)}, u32[]{:S(2)}) async-start(bf16[32,128,256]{2,1,0:T(8,128)(2,1)} %copy.116), calls=%async_computation.1 | async-start | bytes 4194304 | tf_op jit(solution)/shard_map/while/body/eval_jaxpr/all_to_all | solution.py:47
  262.1 31.3 %all-to-all-start.2 = ((bf16[16,128,256]{2,1,0:T(8,128)(2,1)}), bf16[16,128,256]{2,1,0:T(8,128)(2,1)}, u32[]{:S(2)}, u32[]{:S(2)}) async-start(bf16[16,128,256]{2,1,0:T(8,128)(2,1)} %copy.119), calls=%async_computation.2 | async-start | bytes 2097152 | tf_op jit(solution)/shard_map/while/body/eval_jaxpr/all_to_all | solution.py:36
  298.4 57.4 %all-to-all-start.3 = ((bf16[32,128,256]{2,1,0:T(8,128)(2,1)}), bf16[32,128,256]{2,1,0:T(8,128)(2,1)S(1)}, u32[]{:S(2)}, u32[]{:S(2)}) async-start(bf16[32,128,256]{2,1,0:T(8,128)(2,1)} %copy.120), calls=%async_computation.3 | async-start | bytes 4194304 | tf_op jit(solution)/shard_map/while/body/eval_jaxpr/all_to_all | solution.py:47
  408.7 3.4 copy-start.1
  461.0 31.4 %all-to-all-start = ((bf16[16,128,256]{2,1,0:T(8,128)(2,1)}), bf16[16,128,256]{2,1,0:T(8,128)(2,1)}, u32[]{:S(2)}, u32[]{:S(2)}) async-start(bf16[16,128,256]{2,1,0:T(8,128)(2,1)} %copy.115), calls=%async_computation | async-start | bytes 2097152 | tf_op jit(solution)/shard_map/while/body/eval_jaxpr/all_to_all | solution.py:36
  497.3 57.1 %all-to-all-start.1 = ((bf16[32,128,256]{2,1,0:T(8,128)(2,1)}), bf16[32,128,256]{2,1,0:T(8,128)(2,1)S(1)}, u32[]{:S(2)}, u32[]{:S(2)}) async-start(bf16[32,128,256]{2,1,0:T(8,128)(2,1)} %copy.116), calls=%async_computation.1 | async-start | bytes 4194304 | tf_op jit(solution)/shard_map/while/body/eval_jaxpr/all_to_all | solution.py:47
  559.8 31.3 %all-to-all-start.2 = ((bf16[16,128,256]{2,1,0:T(8,128)(2,1)}), bf16[16,128,256]{2,1,0:T(8,128)(2,1)}, u32[]{:S(2)}, u32[]{:S(2)}) async-start(bf16[16,128,256]{2,1,0:T(8,128)(2,1)} %copy.119), calls=%async_computation.2 | async-start | bytes 2097152 | tf_op jit(solution)/shard_map/while/body/eval_jaxpr/all_to_all | solution.py:36
  596.1 57.4 %all-to-all-start.3 = ((bf16[32,128,256]{2,1,0:T(8,128)(2,1)}), bf16[32,128,256]{2,1,0:T(8,128)(2,1)S(1)}, u32[]{:S(2)}, u32[]{:S(2)}) async-start(bf16[32,128,256]{2,1,0:T(8,128)(2,1)} %copy.120), calls=%async_computation.3 | async-start | bytes 4194304 | tf_op jit(solution)/shard_map/while/body/eval_jaxpr/all_to_all | solution.py:47
  706.5 3.4 copy-start.1
where the time goes:
time: 716 us; the launch traced here: 715 us
  waiting for transfers between devices  373 us (52%)
  blocking collectives  185 us (26%)
  starting transfers between devices  72.9 us (10%)
  matrix products  38.4 us (5%)
  local copies, waits for them, and re-layouts  27.6 us (4%)
  other arithmetic  13.7 us (2%)
    all_to_all x5, waiting for transfers between devices, cross_members(): lax.all_to_all(outgoing, MEM, split_axis=0, concat_axis=0, tiled=True)  249 us
    psum x16, blocking collectives, one_axis_at_a_time(): x = lax.psum(x, axis)  185 us
    all_to_all x5, waiting for transfers between devices, cross_groups(): lax.all_to_all(outgoing, GRP, split_axis=0, concat_axis=0, tiled=True)  123 us
    all_to_all x5, starting transfers between devices, cross_members(): lax.all_to_all(outgoing, MEM, split_axis=0, concat_axis=0, tiled=True)  37.8 us
    all_to_all x5, starting transfers between devices, cross_groups(): lax.all_to_all(outgoing, GRP, split_axis=0, concat_axis=0, tiled=True)  35.1 us
    convert_element_type x10, local copies, waits for them, and re-layouts, pack_panels(): jnp.einsum('tk,trh->krh', placing, panels, preferred_element_type=jnp.flo...  19.5 us
    dot_general x10, matrix products, pack_panels(): jnp.einsum('tk,trh->krh', placing, panels, preferred_element_type=jnp.flo...  15 us
  transfers between devices with their start and end apart: 10, of which 10 were waited for; matrix products, arithmetic and copies ran while one was open for 0% of the time, Pallas kernels for 0%

commit v1 on v0

--- a/solution.py
+++ b/solution.py
@@ -12,7 +12,8 @@
 
 def one_axis_at_a_time(x, axes):
     for axis in axes:
-        x = lax.psum(x, axis)
+        parts = lax.all_gather(x, axis)
+        x = jnp.sum(parts, axis=0)
     return x
 
 

time: 716 us -> 762 us (1.064)
  local copies, waits for them, and re-layouts: 27.6 us -> 70.7 us
  other arithmetic: 13.7 us -> 28.1 us
  blocking collectives: 185 us -> 174 us
    psum x16 -> x0, blocking collectives: 185 us -> none  [one_axis_at_a_time(): x = lax.psum(x, axis)]
    while x0 -> x16, blocking collectives: none -> 174 us
    while x4 -> x60, local copies, waits for them, and re-layouts: 0.01 us -> 43.3 us
    reduce_sum x0 -> x24, other arithmetic: none -> 14.4 us  [one_axis_at_a_time(): x = jnp.sum(parts, axis=0)]
  transfers between devices with their start and end apart: 10 -> 10, of which waited for: 10 -> 10; matrix products, arithmetic and copies ran while one was open for 0% -> 1% of each run, Pallas kernels for 0% -> 0%
where the time goes in v1:
time: 762 us; the launch traced here: 759 us
  waiting for transfers between devices  370 us (49%)
  blocking collectives  174 us (23%)
  starting transfers between devices  72.9 us (10%)
  local copies, waits for them, and re-layouts  70.7 us (9%)
  matrix products  38.4 us (5%)
  other arithmetic  28.1 us (4%)
    all_to_all x5, waiting for transfers between devices, cross_members(): lax.all_to_all(outgoing, MEM, split_axis=0, concat_axis=0, tiled=True)  246 us
    while x16, blocking collectives  174 us
    all_to_all x5, waiting for transfers between devices, cross_groups(): lax.all_to_all(outgoing, GRP, split_axis=0, concat_axis=0, tiled=True)  123 us
    while x60, local copies, waits for them, and re-layouts  43.3 us
    all_to_all x5, starting transfers between devices, cross_members(): lax.all_to_all(outgoing, MEM, split_axis=0, concat_axis=0, tiled=True)  37.8 us
    all_to_all x5, starting transfers between devices, cross_groups(): lax.all_to_all(outgoing, GRP, split_axis=0, concat_axis=0, tiled=True)  35.1 us
    convert_element_type x10, local copies, waits for them, and re-layouts, pack_panels(): jnp.einsum('tk,trh->krh', placing, panels, preferred_element_type=jnp.flo...  19.2 us
  transfers between devices with their start and end apart: 10, of which 10 were waited for; matrix products, arithmetic and copies ran while one was open for 1% of the time, Pallas kernels for 0%

profile of v1, /device:TPU:8, one launch (start us, length us, event | category | flops | bytes accessed | tf_op | source)
XLA Modules:
  0.0 759.1 jit_solution(11854337578516530302)
XLA Ops:
  6.2 9.2 %all-to-all-start.4 = ((bf16[16,128,256]{2,1,0:T(8,128)(2,1)}), bf16[16,128,256]{2,1,0:T(8,128)(2,1)S(1)}, u32[]{:S(2)}, u32[]{:S(2)}) async-start(bf16[16,128,256]{2,1,0:T(8,128)(2,1)} %copy.53), calls=%async_computation.4 | async-start | bytes 2097152 | tf_op jit(solution)/shard_map/all_to_all | solution.py:37
  15.5 24.6 %all-to-all-done.4 = bf16[16,128,256]{2,1,0:T(8,128)(2,1)S(1)} async-done(((bf16[16,128,256]{2,1,0:T(8,128)(2,1)}), bf16[16,128,256]{2,1,0:T(8,128)(2,1)S(1)}, u32[]{:S(2)}, u32[]{:S(2)}) %all-to-all-start.4) | async-done | bytes 1048608 | tf_op jit(solution)/shard_map/all_to_all | solution.py:37
  43.9 11.6 %all-to-all-start.5 = ((bf16[32,128,256]{2,1,0:T(8,128)(2,1)}), bf16[32,128,256]{2,1,0:T(8,128)(2,1)S(1)}, u32[]{:S(2)}, u32[]{:S(2)}) async-start(bf16[32,128,256]{2,1,0:T(8,128)(2,1)} %copy.55), calls=%async_computation.5 | async-start | bytes 4194304 | tf_op jit(solution)/shard_map/all_to_all | solution.py:48
  58.9 47.2 %all-to-all-done.5 = bf16[32,128,256]{2,1,0:T(8,128)(2,1)S(1)} async-done(((bf16[32,128,256]{2,1,0:T(8,128)(2,1)}), bf16[32,128,256]{2,1,0:T(8,128)(2,1)S(1)}, u32[]{:S(2)}, u32[]{:S(2)}) %all-to-all-start.5) | async-done | bytes 2097184 | tf_op jit(solution)/shard_map/all_to_all | solution.py:48
  110.1 644.2 %while.16 = (s32[]{:T(128)}, f32[1024,256]{0,1:T(8,128)}, f32[1024,256]{0,1:T(8,128)}, s32[4]{0:T(128)S(1)}, s32[4]{0:T(128)S(1)}, /*index=5*/bf16[1024,512]{1,0...) while((s32[]{:T(128)}, f32[1024,256]{0,1:T(8,128)}, ...), condition=%wide.region_16.17_spmd.clone, body=%wide.region_0.16_spmd.clone.sunk | while | flops 1133779456 | bytes 70787368 | solution.py:111
  114.9 15.9 %all-reduce.36 = f32[8]{0:T(128)S(1)} all-reduce(f32[8]{0:T(128)S(1)} %dynamic-update-slice.36), channel_id=1, replica_groups=mesh['grp_0'=8,'grp_1'=2,'mem_0'=4,'mem_1'=8] {'grp_0'}, use_global_device_ids=true, to_apply=%add | all-reduce | flops 8 | bytes 64 | tf_op jit(solution)/shard_map/while
  139.8 8.5 %all-reduce.38 = f32[4]{0:T(128)S(1)} all-reduce(f32[4]{0:T(128)S(1)} %dynamic-update-slice.38), channel_id=1, replica_groups=mesh['grp_0'=8,'grp_1'=2,'mem_0'=4,'mem_1'=8] {'mem_0'}, use_global_device_ids=true, to_apply=%add.2 | all-reduce | flops 4 | bytes 32 | tf_op jit(solution)/shard_map/while
  151.6 17.9 %all-reduce.39 = f32[8]{0:T(128)S(1)} all-reduce(f32[8]{0:T(128)S(1)} %dynamic-update-slice.39), channel_id=1, replica_groups=mesh['grp_0'=8,'grp_1'=2,'mem_0'=4,'mem_1'=8] {'mem_1'}, use_global_device_ids=true, to_apply=%add.3 | all-reduce | flops 8 | bytes 64 | tf_op jit(solution)/shard_map/while
  181.1 24.7 %all-to-all-done = bf16[16,128,256]{2,1,0:T(8,128)(2,1)} async-done(((bf16[16,128,256]{2,1,0:T(8,128)(2,1)}), bf16[16,128,256]{2,1,0:T(8,128)(2,1)}, u32[]{:S(2)}, u32[]{:S(2)}) %all-to-all-start) | async-done | bytes 1048608 | tf_op jit(solution)/shard_map/while/body/eval_jaxpr/all_to_all | solution.py:37
  216.7 50.5 %all-to-all-done.1 = bf16[32,128,256]{2,1,0:T(8,128)(2,1)S(1)} async-done(((bf16[32,128,256]{2,1,0:T(8,128)(2,1)}), bf16[32,128,256]{2,1,0:T(8,128)(2,1)S(1)}, u32[]{:S(2)}, u32[]{:S(2)}) %all-to-all-start.1) | async-done | bytes 2097184 | tf_op jit(solution)/shard_map/while/body/eval_jaxpr/all_to_all | solution.py:48
  279.1 24.7 %all-to-all-done.2 = bf16[16,128,256]{2,1,0:T(8,128)(2,1)} async-done(((bf16[16,128,256]{2,1,0:T(8,128)(2,1)}), bf16[16,128,256]{2,1,0:T(8,128)(2,1)}, u32[]{:S(2)}, u32[]{:S(2)}) %all-to-all-start.2) | async-done | bytes 1048608 | tf_op jit(solution)/shard_map/while/body/eval_jaxpr/all_to_all | solution.py:37
  317.1 49.2 %all-to-all-done.3 = bf16[32,128,256]{2,1,0:T(8,128)(2,1)S(1)} async-done(((bf16[32,128,256]{2,1,0:T(8,128)(2,1)}), bf16[32,128,256]{2,1,0:T(8,128)(2,1)S(1)}, u32[]{:S(2)}, u32[]{:S(2)}) %all-to-all-start.3) | async-done | bytes 2097184 | tf_op jit(solution)/shard_map/while/body/eval_jaxpr/all_to_all | solution.py:48
  371.6 16.1 %all-reduce.40 = (f32[8]{0:T(128)S(1)}, f32[8]{0:T(128)S(1)}) all-reduce(f32[8]{0:T(128)S(1)} %dynamic-update-slice.40, f32[8]{0:T(128)S(1)} %dynamic-update-slice.41), channel_id=1, replica_groups=mesh['grp_0'=8,'grp_1'=2,'mem_0'=4,'mem_1'=8] {'grp_0'}, use_global_device_ids=true, to_apply=%add.4 | all-reduce | flops 16 | bytes 128 | tf_op jit(solution)/shard_map/while
  398.1 8.8 %all-reduce.42 = (f32[4]{0:T(128)S(1)}, f32[4]{0:T(128)S(1)}) all-reduce(f32[4]{0:T(128)S(1)} %dynamic-update-slice.44, f32[4]{0:T(128)S(1)} %dynamic-update-slice.45), channel_id=1, replica_groups=mesh['grp_0'=8,'grp_1'=2,'mem_0'=4,'mem_1'=8] {'mem_0'}, use_global_device_ids=true, to_apply=%add.6 | all-reduce | flops 8 | bytes 64 | tf_op jit(solution)/shard_map/while
  410.9 17.7 %all-reduce.43 = (f32[8]{0:T(128)S(1)}, f32[8]{0:T(128)S(1)}) all-reduce(f32[8]{0:T(128)S(1)} %dynamic-update-slice.46, f32[8]{0:T(128)S(1)} %dynamic-update-slice.47), channel_id=1, replica_groups=mesh['grp_0'=8,'grp_1'=2,'mem_0'=4,'mem_1'=8] {'mem_1'}, use_global_device_ids=true, to_apply=%add.7 | all-reduce | flops 16 | bytes 128 | tf_op jit(solution)/shard_map/while
  439.1 14.1 %all-reduce.36 = f32[8]{0:T(128)S(1)} all-reduce(f32[8]{0:T(128)S(1)} %dynamic-update-slice.36), channel_id=1, replica_groups=mesh['grp_0'=8,'grp_1'=2,'mem_0'=4,'mem_1'=8] {'grp_0'}, use_global_device_ids=true, to_apply=%add | all-reduce | flops 8 | bytes 64 | tf_op jit(solution)/shard_map/while
  473.3 14.9 %all-reduce.39 = f32[8]{0:T(128)S(1)} all-reduce(f32[8]{0:T(128)S(1)} %dynamic-update-slice.39), channel_id=1, replica_groups=mesh['grp_0'=8,'grp_1'=2,'mem_0'=4,'mem_1'=8] {'mem_1'}, use_global_device_ids=true, to_apply=%add.3 | all-reduce | flops 8 | bytes 64 | tf_op jit(solution)/shard_map/while
  500.3 24.7 %all-to-all-done = bf16[16,128,256]{2,1,0:T(8,128)(2,1)} async-done(((bf16[16,128,256]{2,1,0:T(8,128)(2,1)}), bf16[16,128,256]{2,1,0:T(8,128)(2,1)}, u32[]{:S(2)}, u32[]{:S(2)}) %all-to-all-start) | async-done | bytes 1048608 | tf_op jit(solution)/shard_map/while/body/eval_jaxpr/all_to_all | solution.py:37
  536.7 50.5 %all-to-all-done.1 = bf16[32,128,256]{2,1,0:T(8,128)(2,1)S(1)} async-done(((bf16[32,128,256]{2,1,0:T(8,128)(2,1)}), bf16[32,128,256]{2,1,0:T(8,128)(2,1)S(1)}, u32[]{:S(2)}, u32[]{:S(2)}) %all-to-all-start.1) | async-done | bytes 2097184 | tf_op jit(solution)/shard_map/while/body/eval_jaxpr/all_to_all | solution.py:48
  599.1 24.7 %all-to-all-done.2 = bf16[16,128,256]{2,1,0:T(8,128)(2,1)} async-done(((bf16[16,128,256]{2,1,0:T(8,128)(2,1)}), bf16[16,128,256]{2,1,0:T(8,128)(2,1)}, u32[]{:S(2)}, u32[]{:S(2)}) %all-to-all-start.2) | async-done | bytes 1048608 | tf_op jit(solution)/shard_map/while/body/eval_jaxpr/all_to_all | solution.py:37
  637.1 49.2 %all-to-all-done.3 = bf16[32,128,256]{2,1,0:T(8,128)(2,1)S(1)} async-done(((bf16[32,128,256]{2,1,0:T(8,128)(2,1)}), bf16[32,128,256]{2,1,0:T(8,128)(2,1)S(1)}, u32[]{:S(2)}, u32[]{:S(2)}) %all-to-all-start.3) | async-done | bytes 2097184 | tf_op jit(solution)/shard_map/while/body/eval_jaxpr/all_to_all | solution.py:48
  691.6 16.1 %all-reduce.40 = (f32[8]{0:T(128)S(1)}, f32[8]{0:T(128)S(1)}) all-reduce(f32[8]{0:T(128)S(1)} %dynamic-update-slice.40, f32[8]{0:T(128)S(1)} %dynamic-update-slice.41), channel_id=1, replica_groups=mesh['grp_0'=8,'grp_1'=2,'mem_0'=4,'mem_1'=8] {'grp_0'}, use_global_device_ids=true, to_apply=%add.4 | all-reduce | flops 16 | bytes 128 | tf_op jit(solution)/shard_map/while
  718.1 8.8 %all-reduce.42 = (f32[4]{0:T(128)S(1)}, f32[4]{0:T(128)S(1)}) all-reduce(f32[4]{0:T(128)S(1)} %dynamic-update-slice.44, f32[4]{0:T(128)S(1)} %dynamic-update-slice.45), channel_id=1, replica_groups=mesh['grp_0'=8,'grp_1'=2,'mem_0'=4,'mem_1'=8] {'mem_0'}, use_global_device_ids=true, to_apply=%add.6 | all-reduce | flops 8 | bytes 64 | tf_op jit(solution)/shard_map/while
  730.8 17.7 %all-reduce.43 = (f32[8]{0:T(128)S(1)}, f32[8]{0:T(128)S(1)}) all-reduce(f32[8]{0:T(128)S(1)} %dynamic-update-slice.46, f32[8]{0:T(128)S(1)} %dynamic-update-slice.47), channel_id=1, replica_groups=mesh['grp_0'=8,'grp_1'=2,'mem_0'=4,'mem_1'=8] {'mem_1'}, use_global_device_ids=true, to_apply=%add.7 | all-reduce | flops 16 | bytes 128 | tf_op jit(solution)/shard_map/while
  (175 shorter events, 206.8 us)
Async XLA Ops:
  6.2 33.9 %all-to-all-start.4 = ((bf16[16,128,256]{2,1,0:T(8,128)(2,1)}), bf16[16,128,256]{2,1,0:T(8,128)(2,1)S(1)}, u32[]{:S(2)}, u32[]{:S(2)}) async-start(bf16[16,128,256]{2,1,0:T(8,128)(2,1)} %copy.53), calls=%async_computation.4 | async-start | bytes 2097152 | tf_op jit(solution)/shard_map/all_to_all | solution.py:37
  43.9 11.6 %copy-start.3 = (bf16[1024,256]{1,0:T(8,128)(2,1)S(1)}, bf16[1024,256]{1,0:T(8,128)(2,1)}, u32[]{:S(2)}) copy-start(bf16[1024,256]{1,0:T(8,128)(2,1)} %param.10) | copy-start | bytes 1572868
  43.9 62.1 %all-to-all-start.5 = ((bf16[32,128,256]{2,1,0:T(8,128)(2,1)}), bf16[32,128,256]{2,1,0:T(8,128)(2,1)S(1)}, u32[]{:S(2)}, u32[]{:S(2)}) async-start(bf16[32,128,256]{2,1,0:T(8,128)(2,1)} %copy.55), calls=%async_computation.5 | async-start | bytes 4194304 | tf_op jit(solution)/shard_map/all_to_all | solution.py:48
  106.0 1.3 copy-start.2
  107.3 2.8 copy-start
  107.3 2.8 copy-start.4
  175.0 30.8 %all-to-all-start = ((bf16[16,128,256]{2,1,0:T(8,128)(2,1)}), bf16[16,128,256]{2,1,0:T(8,128)(2,1)}, u32[]{:S(2)}, u32[]{:S(2)}) async-start(bf16[16,128,256]{2,1,0:T(8,128)(2,1)} %copy.115), calls=%async_computation | async-start | bytes 2097152 | tf_op jit(solution)/shard_map/while/body/eval_jaxpr/all_to_all | solution.py:37
  210.8 56.4 %all-to-all-start.1 = ((bf16[32,128,256]{2,1,0:T(8,128)(2,1)}), bf16[32,128,256]{2,1,0:T(8,128)(2,1)S(1)}, u32[]{:S(2)}, u32[]{:S(2)}) async-start(bf16[32,128,256]{2,1,0:T(8,128)(2,1)} %copy.116), calls=%async_computation.1 | async-start | bytes 4194304 | tf_op jit(solution)/shard_map/while/body/eval_jaxpr/all_to_all | solution.py:48
  272.5 31.3 %all-to-all-start.2 = ((bf16[16,128,256]{2,1,0:T(8,128)(2,1)}), bf16[16,128,256]{2,1,0:T(8,128)(2,1)}, u32[]{:S(2)}, u32[]{:S(2)}) async-start(bf16[16,128,256]{2,1,0:T(8,128)(2,1)} %copy.119), calls=%async_computation.2 | async-start | bytes 2097152 | tf_op jit(solution)/shard_map/while/body/eval_jaxpr/all_to_all | solution.py:37
  308.8 57.4 %all-to-all-start.3 = ((bf16[32,128,256]{2,1,0:T(8,128)(2,1)}), bf16[32,128,256]{2,1,0:T(8,128)(2,1)S(1)}, u32[]{:S(2)}, u32[]{:S(2)}) async-start(bf16[32,128,256]{2,1,0:T(8,128)(2,1)} %copy.120), calls=%async_computation.3 | async-start | bytes 4194304 | tf_op jit(solution)/shard_map/while/body/eval_jaxpr/all_to_all | solution.py:48
  431.0 3.4 copy-start.1
  493.7 31.4 %all-to-all-start = ((bf16[16,128,256]{2,1,0:T(8,128)(2,1)}), bf16[16,128,256]{2,1,0:T(8,128)(2,1)}, u32[]{:S(2)}, u32[]{:S(2)}) async-start(bf16[16,128,256]{2,1,0:T(8,128)(2,1)} %copy.115), calls=%async_computation | async-start | bytes 2097152 | tf_op jit(solution)/shard_map/while/body/eval_jaxpr/all_to_all | solution.py:37
  530.1 57.1 %all-to-all-start.1 = ((bf16[32,128,256]{2,1,0:T(8,128)(2,1)}), bf16[32,128,256]{2,1,0:T(8,128)(2,1)S(1)}, u32[]{:S(2)}, u32[]{:S(2)}) async-start(bf16[32,128,256]{2,1,0:T(8,128)(2,1)} %copy.116), calls=%async_computation.1 | async-start | bytes 4194304 | tf_op jit(solution)/shard_map/while/body/eval_jaxpr/all_to_all | solution.py:48
  592.5 31.3 %all-to-all-start.2 = ((bf16[16,128,256]{2,1,0:T(8,128)(2,1)}), bf16[16,128,256]{2,1,0:T(8,128)(2,1)}, u32[]{:S(2)}, u32[]{:S(2)}) async-start(bf16[16,128,256]{2,1,0:T(8,128)(2,1)} %copy.119), calls=%async_computation.2 | async-start | bytes 2097152 | tf_op jit(solution)/shard_map/while/body/eval_jaxpr/all_to_all | solution.py:37
  628.8 57.4 %all-to-all-start.3 = ((bf16[32,128,256]{2,1,0:T(8,128)(2,1)}), bf16[32,128,256]{2,1,0:T(8,128)(2,1)S(1)}, u32[]{:S(2)}, u32[]{:S(2)}) async-start(bf16[32,128,256]{2,1,0:T(8,128)(2,1)} %copy.120), calls=%async_computation.3 | async-start | bytes 4194304 | tf_op jit(solution)/shard_map/while/body/eval_jaxpr/all_to_all | solution.py:48
  751.0 3.4 copy-start.1
